TPU v7x, 32 devices: a whole 2x2x4 slice. The times are simulated.
32 devices in a mesh: groups: 2 (over x), seq: 8 (over z, y), batch: 2 (over core).
Axes of the slice: x: 2, y: 2, z: 4, core: 2. Of those that a mesh axis runs over, the one named last changes fastest.
Arguments:
- prompt_cache: bfloat16 [16, 256, 8, 256], P(('groups', 'batch'), 'seq'), parts along dimension 0, may hold values from -6 to 6
- prompt_states: float32 [16, 8, 16, 16384], P(('groups', 'batch'), 'seq'), parts along dimension 0, may hold values from -6 to 6
- block_steps: float32 [16, 8, 16384], P(('groups', 'batch'), 'seq'), parts along dimension 0, may hold values from 0.005 to 0.1
- prompt_lengths: int32 [16], P('groups'), parts along dimension 0, may hold values from 42 to 255
- target_slots: int32 [16], P('groups'), parts along dimension 0, may hold values from 0 to 15, as said below
- cache_lengths: int32 [32], P(('groups', 'batch')), parts along dimension 0, may hold values from 42 to 255
- resident_cache: bfloat16 [32, 32, 8, 8, 256], P(('groups', 'batch'), None, 'seq'), parts along dimension 0, may hold values from -6 to 6
- token_cache: bfloat16 [32, 8, 256], P(('groups', 'batch')), parts along dimension 0, may hold values from -6 to 6
- queries: bfloat16 [32, 64, 128], P(('groups', 'batch')), parts along dimension 0, may hold values from -6 to 6
- resident_states: float32 [32, 16, 16384], P(('groups', 'batch'), None, 'seq'), parts along dimension 0, may hold values from -6 to 6
- decay_rates: float32 [16, 16384], replicated, may hold values from 0.05 to 10
- step_sizes: float32 [32, 16384], P(('groups', 'batch'), 'seq'), parts along dimension 0, may hold values from 0.01 to 1
- inner_input: bfloat16 [32, 16384], P(('groups', 'batch'), 'seq'), parts along dimension 0, may hold values from -6 to 6
- inner_gate: bfloat16 [32, 16384], P(('groups', 'batch'), 'seq'), parts along dimension 0, may hold values from -6 to 6
- state_input: float32 [32, 16], P(('groups', 'batch')), parts along dimension 0, may hold values from -6 to 6
- state_readout: float32 [32, 16], P(('groups', 'batch')), parts along dimension 0, may hold values from -6 to 6
- skip_gain: float32 [16384], P('seq'), may hold values from 0.5 to 1.5
Outputs:
- merged_cache: bfloat16 [32, 32, 8, 8, 256], P(('groups', 'batch'), None, 'seq'), parts along dimension 0
- attention: bfloat16 [32, 64, 128], P(('groups', 'batch'), 'seq'), parts along dimension 0
- next_states: float32 [32, 16, 16384], P(('groups', 'batch'), None, 'seq'), parts along dimension 0
- mamba_output: bfloat16 [32, 16384], P(('groups', 'batch'), 'seq'), parts along dimension 0
There are 2 independent parts, one for each index of `groups`. A program takes and returns all parts, laid end to end along the dimension named above; an argument that names none is the same for every part. Nothing has to cross between parts.
Inputs may be any that keep to these rules, and one draw needn't show every extreme that they name: `target_slots`: 8 distinct slots.
All inputs are finite; a program needn't handle non-finite values.
Results may differ from a plain program's by a relative error of at most 0.0019.
Values may be sent and summed in bfloat16 or wider, within the bound.
A program may use at most 320 MiB of HBM per device.

v0:
```python
import math

import jax
import jax.numpy as jnp
from jax import lax
from jax.sharding import PartitionSpec as P


def carried_in(shard, axis, combine, identity):
    count, position = (lax.axis_size(axis), lax.axis_index(axis))
    everything = lax.all_gather(shard, axis)
    start = jnp.broadcast_to(jnp.asarray(identity, shard.dtype), shard.shape)

    def step(k, before):
        at = count - 1 - k
        reached = at > position
        new = combine(before, everything[at])
        return jnp.where(reached, new, before)

    return lax.fori_loop(0, count, step, start)


def add_terms(earlier, latter):
    return earlier + latter


def to_cyclic(blocks, seq_count):
    count, length, heads, width = blocks.shape
    return blocks.reshape(count, length // seq_count, seq_count, heads, width)


def block_usable(lengths, seq_index, block_len):
    return (seq_index * block_len < lengths).astype(jnp.float32)


def decay_term(states, behind, usable, rates):
    return usable[:, None, None] * jnp.exp(-rates[None] * behind[:, None, :]) * states


def local(
    prompt_cache,
    prompt_states,
    block_steps,
    prompt_lengths,
    target_slots,
    cache_lengths,
    resident_cache,
    token_cache,
    queries,
    resident_states,
    decay_rates,
    step_sizes,
    inner_input,
    inner_gate,
    state_input,
    state_readout,
    skip_gain,
):
    seq_count = lax.axis_size("seq")
    seq_index = lax.axis_index("seq")
    batch_index = lax.axis_index("batch")
    local_prompts, block_len, kv_heads, kv_width = prompt_cache.shape
    head_dim = kv_width // 2
    requests = resident_cache.shape[0]
    channels = decay_rates.shape[1]
    local_channels = channels // seq_count
    every_cache = lax.all_gather(prompt_cache, "batch", axis=0, tiled=True)
    every_states, every_steps = (
        lax.all_gather(prompt_states, "batch", axis=0, tiled=True),
        lax.all_gather(block_steps, "batch", axis=0, tiled=True),
    )
    usable = block_usable(prompt_lengths, seq_index, block_len)
    moved = lax.all_to_all(
        to_cyclic(every_cache, seq_count), "seq", split_axis=2, concat_axis=1, tiled=True
    )
    step_terms = every_steps[:, 0, :] * usable[:, None]
    behind = carried_in(step_terms, "seq", add_terms, jnp.zeros_like(step_terms))
    handed = lax.psum_scatter(
        decay_term(every_states[:, 0], behind, usable, decay_rates),
        "seq",
        scatter_dimension=2,
        tiled=True,
    )
    arrived = moved[:, :, 0]
    prompt_count = arrived.shape[0]
    slot_ids = batch_index * requests + jnp.arange(requests, dtype=jnp.int32)
    matches = target_slots[None, :] == slot_ids[:, None]
    fresh = jnp.any(matches, axis=1)
    chosen_len = jnp.sum(jnp.where(matches, prompt_lengths[None, :], 0), axis=1)
    lengths = jnp.where(fresh, chosen_len, cache_lengths)
    picked = jnp.dot(
        matches.astype(jnp.bfloat16),
        arrived.reshape(prompt_count, -1),
        preferred_element_type=jnp.float32,
    )
    picked = picked.astype(jnp.bfloat16).reshape(requests, block_len, kv_heads, kv_width)
    position = jnp.arange(block_len, dtype=jnp.int32) * seq_count + seq_index
    merged = jnp.where(fresh[:, None, None, None], picked, resident_cache[:, :, 0])
    merged = jnp.where(
        (position[None, :] < lengths[:, None])[:, :, None, None],
        merged,
        jnp.zeros((), jnp.bfloat16),
    )
    merged = jnp.where(
        (position[None, :] == lengths[:, None])[:, :, None, None], token_cache[:, None], merged
    )
    heads = queries.shape[1]
    group = heads // kv_heads
    grouped = queries.reshape(requests, kv_heads, group, head_dim)
    scores = jnp.einsum(
        "rgqd,rtgd->rgqt", grouped, merged[..., :head_dim], preferred_element_type=jnp.float32
    ) * (1.0 / math.sqrt(head_dim))
    seen = (position[None, :] <= lengths[:, None])[:, None, None, :]
    masked = jnp.where(seen, scores, -1e30)
    highest = jnp.max(masked, axis=3)
    weights = jnp.where(seen, jnp.exp(masked - highest[..., None]), 0.0)
    denominator = jnp.sum(weights, axis=3)
    summed = jnp.einsum(
        "rgqt,rtgd->rgqd",
        weights.astype(jnp.bfloat16),
        merged[..., head_dim:],
        preferred_element_type=jnp.float32,
    )
    highest = highest.reshape(requests, heads)
    denominator = denominator.reshape(requests, heads)
    summed = summed.reshape(requests, heads, head_dim)
    peer_top, peer_total, peer_sum = (
        lax.all_to_all(highest[:, None], "seq", split_axis=2, concat_axis=1, tiled=True),
        lax.all_to_all(denominator[:, None], "seq", split_axis=2, concat_axis=1, tiled=True),
        lax.all_to_all(summed[:, None], "seq", split_axis=2, concat_axis=1, tiled=True),
    )
    common_top = jnp.max(peer_top, axis=1)
    factor = jnp.exp(peer_top - common_top[:, None])
    owner_total = jnp.sum(peer_total * factor, axis=1)
    owner_sum = jnp.sum(peer_sum * factor[..., None], axis=1)
    attention = (owner_sum / owner_total[..., None]).astype(jnp.bfloat16)
    rates_here = lax.dynamic_slice_in_dim(
        decay_rates, seq_index * local_channels, local_channels, 1
    )
    chosen_state = jnp.einsum(
        "rp,pnc->rnc", matches.astype(jnp.float32), handed, precision=lax.Precision.HIGHEST
    )
    start = jnp.where(fresh[:, None, None], chosen_state, resident_states)
    inner = inner_input.astype(jnp.float32)
    next_states = (
        jnp.exp(-rates_here[None] * step_sizes[:, None, :]) * start
        + (step_sizes * inner)[:, None, :] * state_input[:, :, None]
    )
    readout = jnp.sum(state_readout[:, :, None] * next_states, axis=1) + skip_gain[None, :] * inner
    mamba_output = (readout * jax.nn.silu(inner_gate.astype(jnp.float32))).astype(jnp.bfloat16)
    return (merged[:, :, None], attention, next_states, mamba_output)


def solution(mesh):
    return jax.shard_map(
        local,
        mesh=mesh,
        in_specs=(
            P(("groups", "batch"), "seq", None, None),
            P(("groups", "batch"), "seq", None, None),
            P(("groups", "batch"), "seq", None),
            P("groups"),
            P("groups"),
            P(("groups", "batch")),
            P(("groups", "batch"), None, "seq", None, None),
            P(("groups", "batch"), None, None),
            P(("groups", "batch"), None, None),
            P(("groups", "batch"), None, "seq"),
            P(),
            P(("groups", "batch"), "seq"),
            P(("groups", "batch"), "seq"),
            P(("groups", "batch"), "seq"),
            P(("groups", "batch"), None),
            P(("groups", "batch"), None),
            P("seq"),
        ),
        out_specs=(
            P(("groups", "batch"), None, "seq", None, None),
            P(("groups", "batch"), "seq", None),
            P(("groups", "batch"), None, "seq"),
            P(("groups", "batch"), "seq"),
        ),
        check_vma=False,
    )
```

profile of v0, /device:TPU:0, one launch (start us, length us, event | category | flops | bytes accessed | tf_op | source)
XLA Modules:
  0.0 312.2 jit_solution(4913443548733190569)
XLA Ops:
  7.2 2.6 all_gather.14
  9.9 0.7 compare_convert_fusion
  11.0 1.1 copy.61
  12.2 0.7 all-gather.8.cloned.1.call-update
  12.9 0.7 all-gather.4.cloned.1.call-update
  13.8 73.9 %all-gather.6.cloned.1.call-done = f32[8,8,16384]{2,1,0:T(8,128)} async-done(((f32[1,8,16384]{2,1,0:T(8,128)}), f32[8,8,16384]{2,1,0:T(8,128)}) %all-gather.6.cloned.1.call-update) | async-done | bytes 4194320 | tf_op jit(solution)/shard_map/all_gather | solution.py:11
  87.7 9.9 %while.16 = (s32[]{:T(128)}, f32[8,16384]{1,0:T(8,128)S(1)}, s32[]{:T(128)}, f32[8,8,16384]{2,1,0:T(8,128)}, s32[]{:T(128)}, /*index=5*/s32[]{:T(128)}, s32[]{:T(128)}, s32[]{:T(128)}) while((s32[]{:T(128)}, f32[8,16384]{1,0:T(8,128)S(1)}, s32[]{:T(128)}, f32[8,8,16384]{2,1,0:T(8,128)}, s32[]{:T(128)}, /*index=5*/s32[]{:T(128)}, ...), condition=%wide.region_8.9_spmd.clone, body=%wide.region_7.8_spmd.clone.sunk | while | flops 393224 | bytes 1573027 | solution.py:20
  87.7 1.2 add_select_fusion.2
  88.9 1.2 add_select_fusion.2
  90.1 1.2 add_select_fusion.2
  91.3 1.2 add_select_fusion.2
  92.5 1.2 add_select_fusion.2
  93.7 1.3 add_select_fusion.2
  95.0 1.3 add_select_fusion.2
  96.3 1.3 add_select_fusion.2
  97.6 10.0 %all-gather.8.cloned.1.call-done = f32[8,1,16,16384]{3,2,1,0:T(8,128)} async-done(((f32[4,1,16,16384]{3,2,1,0:T(8,128)}), f32[8,1,16,16384]{3,2,1,0:T(8,128)}) %all-gather.8.cloned.1.call-update) | async-done | bytes 8388624 | tf_op jit(solution)/shard_map/all_gather | solution.py:69
  107.6 6.2 %bitcast_multiply_fusion = f32[8,16,16384]{2,1,0:T(8,128)} fusion(f32[8,1,16,16384]{3,2,1,0:T(8,128)} %all-gather.8.cloned.1.call-done, f32[8,16384]{1,0:T(8,128)S(1)} %get-tuple-element.114, f32[16,16384]{1,0:T(8,128)S(1)} %neg.13, f32[8]{0:T(128)S(1)} %compare_convert_fusion), kind=kLoop, calls=%fused_computation.2 | loop fusion | flops 6291456 | bytes 18350112 | tf_op jit(solution)/shard_map/mul | solution.py:37
  113.9 5.5 %all-gather.4.cloned.1.call-done = bf16[8,32,8,256]{3,2,1,0:T(8,128)(2,1)} async-done(((bf16[4,32,8,256]{3,2,1,0:T(8,128)(2,1)}), bf16[8,32,8,256]{3,2,1,0:T(8,128)(2,1)}) %all-gather.4.cloned.1.call-update) | async-done | bytes 1048592 | tf_op jit(solution)/shard_map/all_gather | solution.py:67
  119.4 2.3 copy.53
  121.7 5.8 %all-to-all-start = ((bf16[8,4,8,8,256]{4,3,1,0,2:T(8,128)(2,1)}), bf16[8,4,8,8,256]{4,3,1,0,2:T(8,128)(2,1)S(1)}, u32[]{:S(2)}, u32[]{:S(2)}) async-start(bf16[8,4,8,8,256]{4,3,1,0,2:T(8,128)(2,1)} %copy.53), calls=%async_computation | async-start | bytes 2097152 | tf_op jit(solution)/shard_map/all_to_all | solution.py:73
  128.1 0.6 convert_multiply_fusion.2
  128.7 48.5 %all-to-all-done = bf16[8,4,8,8,256]{4,3,1,0,2:T(8,128)(2,1)S(1)} async-done(((bf16[8,4,8,8,256]{4,3,1,0,2:T(8,128)(2,1)}), bf16[8,4,8,8,256]{4,3,1,0,2:T(8,128)(2,1)S(1)}, u32[]{:S(2)}, u32[]{:S(2)}) %all-to-all-start) | async-done | bytes 1048608 | tf_op jit(solution)/shard_map/all_to_all | solution.py:73
  177.3 1.4 reshape_squeeze.3
  178.8 1.7 convolution_convert_fusion
  180.5 1.4 fusion.5
  182.0 0.5 fusion.31
  182.4 0.6 copy-done.3
  183.0 0.9 fusion.11
  183.9 1.4 copy.68
  185.4 5.9 %all-to-all-start.3 = ((f32[8,1,64]{0,1,2:T(1,128)}), f32[8,1,64]{0,1,2:T(1,128)}, u32[]{:S(2)}, u32[]{:S(2)}) async-start(f32[8,1,64]{0,1,2:T(1,128)} %bitcast.50), calls=%async_computation.3 | async-start | bytes 65536 | tf_op jit(solution)/shard_map/all_to_all | solution.py:129
  191.3 1.6 dynamic-slice_negate_fusion
  193.0 0.8 copy.64
  193.8 1.4 copy.59
  195.2 3.5 %all-to-all-done.3 = f32[8,1,64]{0,1,2:T(1,128)} async-done(((f32[8,1,64]{0,1,2:T(1,128)}), f32[8,1,64]{0,1,2:T(1,128)}, u32[]{:S(2)}, u32[]{:S(2)}) %all-to-all-start.3) | async-done | bytes 2080 | tf_op jit(solution)/shard_map/all_to_all | solution.py:129
  198.7 3.9 %all-to-all-start.2 = ((f32[8,1,64]{0,1,2:T(1,128)}), f32[8,1,64]{0,1,2:T(1,128)}, u32[]{:S(2)}, u32[]{:S(2)}) async-start(f32[8,1,64]{0,1,2:T(1,128)} %bitcast.49), calls=%async_computation.2 | async-start | bytes 65536 | tf_op jit(solution)/shard_map/all_to_all | solution.py:128
  202.6 1.1 convolution_bitcast_fusion
  203.8 0.9 copy.58
  204.6 5.3 %all-to-all-done.2 = f32[8,1,64]{0,1,2:T(1,128)} async-done(((f32[8,1,64]{0,1,2:T(1,128)}), f32[8,1,64]{0,1,2:T(1,128)}, u32[]{:S(2)}, u32[]{:S(2)}) %all-to-all-start.2) | async-done | bytes 2080 | tf_op jit(solution)/shard_map/all_to_all | solution.py:128
  209.9 3.4 %all-to-all-start.1 = ((f32[8,1,64,128]{3,0,1,2:T(8,128)}), f32[8,1,64,128]{3,0,1,2:T(8,128)S(1)}, u32[]{:S(2)}, u32[]{:S(2)}) async-start(f32[8,1,64,128]{3,0,1,2:T(8,128)} %copy.58), calls=%async_computation.1 | async-start | bytes 524288 | tf_op jit(solution)/shard_map/all_to_all | solution.py:130
  213.3 2.3 fusion.8
  215.6 0.8 reduce_max.19
  216.4 0.8 multiply_reduce_fusion.2
  217.2 8.3 %all-to-all-done.1 = f32[8,1,64,128]{3,0,1,2:T(8,128)S(1)} async-done(((f32[8,1,64,128]{3,0,1,2:T(8,128)}), f32[8,1,64,128]{3,0,1,2:T(8,128)S(1)}, u32[]{:S(2)}, u32[]{:S(2)}) %all-to-all-start.1) | async-done | bytes 262176 | tf_op jit(solution)/shard_map/all_to_all | solution.py:130
  225.7 0.6 copy.66
  226.4 73.6 %reduce-scatter.2.cloned.1.call-done = f32[8,16,2048]{2,1,0:T(8,128)} async-done(((f32[8,16,16384]{2,1,0:T(8,128)}), f32[8,16,2048]{2,1,0:T(8,128)}) %reduce-scatter.2.cloned.1.call-update) | async-done | bytes 1048592 | tf_op jit(solution)/shard_map/reduce_scatter | solution.py:78
  299.9 3.5 %multiply_reduce_fusion = (f32[8,2048]{1,0:T(8,128)S(1)}, f32[8,16,2048]{2,0,1:T(8,128)S(1)}) fusion(f32[8,16]{0,1:T(8,128)S(1)} %copy.65, f32[8,16]{0,1:T(8,128)S(1)} %copy.64, f32[8,2048]{1,0:T(8,128)} %convert_multiply_fusion.2, f32[8,16,2048]{2,1,0:T(8,128)} %param.28, f32[8,16,2048]{2,1,0:T(8,128)} %reduce-scatter.2.cloned.1.call-done, s32[8]{0:T(128)} %param.23, ...), kind=kOutput, calls=%fused_computation.17 | convolution fusion | flops 26984512 | bytes 3474504 | tf_op jit(solution)/shard_map/rp,pnc->rnc/dot_general | solution.py:140
  303.4 1.6 copy.67
  305.0 0.7 fusion.20
  (56 shorter events, 1.6 us)
Async XLA Ops:
  7.2 174.8 %copy-start = (bf16[8,64,128]{2,1,0:T(8,128)(2,1)S(1)}, bf16[8,64,128]{2,1,0:T(8,128)(2,1)}, u32[]{:S(2)}) copy-start(bf16[8,64,128]{2,1,0:T(8,128)(2,1)} %param.27) | copy-start | bytes 393220
  7.2 6.5 %copy-start.2 = (f32[16,16384]{1,0:T(8,128)S(1)}, f32[16,16384]{1,0:T(8,128)}, u32[]{:S(2)}) copy-start(f32[16,16384]{1,0:T(8,128)} %param.29) | copy-start | bytes 3145732
  7.2 80.5 %all-gather.6.cloned.1.call-start = ((), (), s32[]{:S(2)}) async-start(), calls=%async_computation.6 | async-start | bytes 4718592 | tf_op jit(solution)/shard_map/all_gather | solution.py:11
  12.1 95.5 %all-gather.8.cloned.1.call-start = ((), (), s32[]{:S(2)}) async-start(), calls=%async_computation.7 | async-start | bytes 12582912 | tf_op jit(solution)/shard_map/all_gather | solution.py:69
  12.9 106.5 %all-gather.4.cloned.1.call-start = ((), (), s32[]{:S(2)}) async-start(), calls=%async_computation.5 | async-start | bytes 1572864 | tf_op jit(solution)/shard_map/all_gather | solution.py:67
  13.6 286.3 %reduce-scatter.2.cloned.1.call-start = ((), (), s32[]{:S(2)}) async-start(), calls=%async_computation.8 | async-start | bytes 9437184 | tf_op jit(solution)/shard_map/reduce_scatter | solution.py:78
  113.8 13.7 %copy-start.14 = (s32[8]{0:T(128)S(1)}, s32[8]{0:T(128)}, u32[]{:S(2)}) copy-start(s32[8]{0:T(128)} %param.23) | copy-start | bytes 100
  113.8 13.9 %copy-start.17 = (s32[8]{0:T(128)S(1)}, s32[8]{0:T(128)}, u32[]{:S(2)}) copy-start(s32[8]{0:T(128)} %param.22) | copy-start | bytes 100
  113.8 14.1 %copy-start.18 = (s32[8]{0:T(128)S(1)}, s32[8]{0:T(128)}, u32[]{:S(2)}) copy-start(s32[8]{0:T(128)} %param.24) | copy-start | bytes 100
  113.8 14.2 %copy-start.4 = (f32[8,2048]{1,0:T(8,128)S(1)}, f32[8,2048]{1,0:T(8,128)}, u32[]{:S(2)}) copy-start(f32[8,2048]{1,0:T(8,128)} %param.30) | copy-start | bytes 196612
  113.8 14.2 %copy-start.6 = (bf16[8,2048]{1,0:T(8,128)(2,1)S(1)}, bf16[8,2048]{1,0:T(8,128)(2,1)}, u32[]{:S(2)}) copy-start(bf16[8,2048]{1,0:T(8,128)(2,1)} %param.31) | copy-start | bytes 98308
  113.8 66.7 %copy-start.1 = (bf16[8,32,1,8,256]{4,3,2,1,0:T(8,128)(2,1)S(1)}, bf16[8,32,1,8,256]{4,3,2,1,0:T(8,128)(2,1)}, u32[]{:S(2)}) copy-start(bf16[8,32,1,8,256]{4,3,2,1,0:T(8,128)(2,1)} %param.25) | copy-start | bytes 3145732
  113.8 66.7 %copy-start.5 = (bf16[8,8,256]{2,1,0:T(8,128)(2,1)S(1)}, bf16[8,8,256]{2,1,0:T(8,128)(2,1)}, u32[]{:S(2)}) copy-start(bf16[8,8,256]{2,1,0:T(8,128)(2,1)} %param.26) | copy-start | bytes 98308
  113.9 79.0 %copy-start.16 = (f32[8,16]{1,0:T(8,128)S(1)}, f32[8,16]{1,0:T(8,128)}, u32[]{:S(2)}) copy-start(f32[8,16]{1,0:T(8,128)} %param.34) | copy-start | bytes 1540
  121.7 55.5 %all-to-all-start = ((bf16[8,4,8,8,256]{4,3,1,0,2:T(8,128)(2,1)}), bf16[8,4,8,8,256]{4,3,1,0,2:T(8,128)(2,1)S(1)}, u32[]{:S(2)}, u32[]{:S(2)}) async-start(bf16[8,4,8,8,256]{4,3,1,0,2:T(8,128)(2,1)} %copy.53), calls=%async_computation | async-start | bytes 2097152 | tf_op jit(solution)/shard_map/all_to_all | solution.py:73
  127.5 54.4 %copy-start.15 = (s32[8]{0:T(128)}, s32[8]{0:T(128)S(1)}, u32[]{:S(2)}) copy-start(s32[8]{0:T(128)S(1)} %iota_add_fusion) | copy-start | bytes 100
  127.7 54.2 %copy-start.13 = (pred[8]{0:T(512)(128)(4,1)}, pred[8]{0:T(512)(128)(4,1)S(1)}, u32[]{:S(2)}) copy-start(pred[8]{0:T(512)(128)(4,1)S(1)} %compare_reduce_fusion) | copy-start | bytes 28
  128.0 53.9 %copy-start.9 = (pred[8,32]{1,0:T(8,128)(4,1)}, pred[8,32]{1,0:T(8,128)(4,1)S(1)}, u32[]{:S(2)}) copy-start(pred[8,32]{1,0:T(8,128)(4,1)S(1)} %get-tuple-element.157) | copy-start | bytes 772
  128.1 53.9 %copy-start.10 = (pred[8,32]{1,0:T(8,128)(4,1)}, pred[8,32]{1,0:T(8,128)(4,1)S(1)}, u32[]{:S(2)}) copy-start(pred[8,32]{1,0:T(8,128)(4,1)S(1)} %get-tuple-element.158) | copy-start | bytes 772
  128.1 63.3 %copy-start.11 = (pred[8,32]{1,0:T(8,128)(4,1)}, pred[8,32]{1,0:T(8,128)(4,1)S(1)}, u32[]{:S(2)}) copy-start(pred[8,32]{1,0:T(8,128)(4,1)S(1)} %get-tuple-element.156) | copy-start | bytes 772
  182.4 0.6 copy-start.3
  185.4 13.3 %all-to-all-start.3 = ((f32[8,1,64]{0,1,2:T(1,128)}), f32[8,1,64]{0,1,2:T(1,128)}, u32[]{:S(2)}, u32[]{:S(2)}) async-start(f32[8,1,64]{0,1,2:T(1,128)} %bitcast.50), calls=%async_computation.3 | async-start | bytes 65536 | tf_op jit(solution)/shard_map/all_to_all | solution.py:129
  198.7 11.2 %all-to-all-start.2 = ((f32[8,1,64]{0,1,2:T(1,128)}), f32[8,1,64]{0,1,2:T(1,128)}, u32[]{:S(2)}, u32[]{:S(2)}) async-start(f32[8,1,64]{0,1,2:T(1,128)} %bitcast.49), calls=%async_computation.2 | async-start | bytes 65536 | tf_op jit(solution)/shard_map/all_to_all | solution.py:128
  203.7 101.3 %copy-start.7 = (bf16[8,2048]{1,0:T(8,128)(2,1)S(1)}, bf16[8,2048]{1,0:T(8,128)(2,1)}, u32[]{:S(2)}) copy-start(bf16[8,2048]{1,0:T(8,128)(2,1)} %param.31) | copy-start | bytes 98308
  203.7 101.3 %copy-start.8 = (bf16[8,2048]{1,0:T(8,128)(2,1)S(1)}, bf16[8,2048]{1,0:T(8,128)(2,1)}, u32[]{:S(2)}) copy-start(bf16[8,2048]{1,0:T(8,128)(2,1)} %param.32) | copy-start | bytes 98308
  203.7 101.3 %copy-start.12 = (f32[2048]{0:T(1024)S(1)}, f32[2048]{0:T(1024)}, u32[]{:S(2)}) copy-start(f32[2048]{0:T(1024)} %param.35) | copy-start | bytes 24580
  209.9 15.6 %all-to-all-start.1 = ((f32[8,1,64,128]{3,0,1,2:T(8,128)}), f32[8,1,64,128]{3,0,1,2:T(8,128)S(1)}, u32[]{:S(2)}, u32[]{:S(2)}) async-start(f32[8,1,64,128]{3,0,1,2:T(8,128)} %copy.58), calls=%async_computation.1 | async-start | bytes 524288 | tf_op jit(solution)/shard_map/all_to_all | solution.py:130
Sparse Core Ops, SparseCore 0:
  12.2 75.3 all-gather.5
  89.2 18.3 all-gather.7
  109.2 10.1 all-gather.3
  122.9 176.9 reduce-scatter.1
where the time goes:
time: 314 us; the launch traced here: 312 us
  waiting for transfers between devices  230 us (73%)
  other arithmetic  26.8 us (9%)
  starting transfers between devices  19.2 us (6%)
  between operations  14.1 us (4%)
  local copies, waits for them, and re-layouts  12.4 us (4%)
  matrix products  6.71 us (2%)
    all_gather x1, waiting for transfers between devices, carried_in(): everything = lax.all_gather(shard, axis)  73.9 us
    reduce_scatter x1, waiting for transfers between devices, local(): lax.psum_scatter(decay_term(every_states[:, 0], behind, usable, decay_rat...  73.6 us
    all_to_all x1, waiting for transfers between devices, local(): lax.all_to_all(to_cyclic(every_cache, seq_count), 'seq', split_axis=2, co...  48.5 us
    all_gather x1, waiting for transfers between devices, local(): lax.all_gather(prompt_states, 'batch', axis=0, tiled=True)  10 us
    select_n x8, other arithmetic, step(): return jnp.where(reached, new, before)  9.73 us
    all_to_all x1, waiting for transfers between devices, local(): lax.all_to_all(summed[:, None], 'seq', split_axis=2, concat_axis=1, tiled...  8.33 us
  transfers between devices with their start and end apart: 8, of which 8 were waited for; matrix products, arithmetic and copies ran while one was open for 12% of the time, Pallas kernels for 0%

commit v1 on v0

v1 whole, which is shorter than its diff:
```python
import functools
import math

import jax
import jax.numpy as jnp
from jax import lax
from jax.experimental import pallas as pl
from jax.experimental.pallas import tpu as pltpu
from jax.sharding import PartitionSpec as P

MESH = pl.DeviceIdType.MESH
FULL = 32760.0
LOW = -1e30


def kernel(
    dims,
    plen,
    tslot,
    clen,
    cache,
    states,
    steps,
    resident,
    token,
    queries,
    rstates,
    rates,
    dt,
    inner,
    gate,
    s_in,
    s_out,
    skip,
    merged,
    attention,
    nstates,
    mout,
    arrived,
    cache_send,
    handed,
    acc,
    osend,
    orecv,
    lse_send,
    lse_recv,
    *rest,
):
    n, nb, levels, block_len = dims
    d_send, d_recv, d_sel, d_cur, q_send, q_recv, m_send, m_recv = (
        rest[i * levels : (i + 1) * levels] for i in range(8)
    )
    (
        cache_ss, cache_rs, relay_ss, relay_rs, d_ss, d_rs, q_ss, q_rs, m_ss, m_rs,
        hand_ss, hand_rs, o_ss, o_rs, l_ss, l_rs,
    ) = rest[8 * levels :]
    me = lax.axis_index("seq")
    b = lax.axis_index("batch")
    prompts, rows, _, kv_heads, width = cache.shape
    all_prompts = prompts * nb
    requests, heads, head_dim = queries.shape
    state_n, channels = rates.shape
    share_len = channels // n
    chunk = min(512, share_len)
    per_share = share_len // chunk
    own_heads = heads // n
    group = heads // kv_heads
    positions = resident.shape[1]
    bits = [lax.rem(me // (1 << s), 2) for s in range(levels)]
    peers = [me + (1 - 2 * bits[s]) * (1 << s) for s in range(levels)]
    first = b * prompts

    def remote(src, dst, ss, rs, where):
        return pltpu.make_async_remote_copy(
            src_ref=src, dst_ref=dst, send_sem=ss, recv_sem=rs, device_id=where, device_id_type=MESH
        )

    barrier = pltpu.get_barrier_semaphore()
    for k in range(1, n):
        pl.semaphore_signal(
            barrier, inc=1, device_id={"seq": lax.rem(me + k, n)}, device_id_type=MESH
        )
    for k in range(1, nb):
        pl.semaphore_signal(
            barrier, inc=1, device_id={"batch": lax.rem(b + k, nb)}, device_id_type=MESH
        )
    pl.semaphore_wait(barrier, n - 1 + nb - 1)

    usable = [
        jnp.where(me * block_len < plen[first + p], 1.0, 0.0).astype(jnp.float32)
        for p in range(prompts)
    ]
    row_id = lax.broadcasted_iota(jnp.int32, (prompts, share_len), 0)
    usable_rows = jnp.zeros((prompts, share_len), jnp.float32)
    for p in range(prompts):
        usable_rows = jnp.where(row_id == p, usable[p], usable_rows)

    def lanes(share, c=0, size=share_len):
        return pl.ds(pl.multiple_of(share * share_len + c * chunk, 128), size)

    pending = []

    def start(copy):
        copy.start()
        pending.append(copy)
        return copy

    @pl.loop(0, n // 2)
    def _(k):
        d_send[0][k] = steps[:, lanes(2 * k + 1 - bits[0])] * usable_rows

    d_copies = [
        remote(
            d_send[s].at[pl.ds(0, n >> (s + 1))],
            d_recv[s].at[pl.ds(0, n >> (s + 1))],
            d_ss.at[s],
            d_rs.at[s],
            {"seq": peers[s]},
        )
        for s in range(levels)
    ]
    start(d_copies[0])

    @pl.loop(0, n)
    def _(to):
        cache_send[to] = cache[:, :, to]

    cache_copies = []
    for k in range(1, n):
        to = lax.rem(me + k, n)
        cache_copies.append(
            start(
                remote(
                    cache_send.at[to],
                    arrived.at[b, me],
                    cache_ss.at[k - 1],
                    cache_rs.at[k - 1],
                    {"seq": to},
                )
            )
        )
    arrived[b, me] = cache[:, :, me]

    def read(s, p, k, c):
        if s == 0:
            share = k
            return states[p, :, lanes(share, c, chunk)] * usable[p]
        return acc[p, k, :, pl.ds(pl.multiple_of(c * chunk, 128), chunk)]

    q_copies, m_copies = {}, {}

    def send_half(s, p):
        count = (n >> (s + 1)) * per_share

        def largest(i, top):
            k, c = i // per_share, lax.rem(i, per_share)
            return jnp.maximum(top, jnp.abs(read(s, p, 2 * k + 1 - bits[s], c)))

        top = lax.fori_loop(0, count, largest, jnp.full((state_n, chunk), 1e-30, jnp.float32))
        top = jnp.max(jnp.max(top, axis=0, keepdims=True), axis=1, keepdims=True)
        m_send[s][p] = jnp.broadcast_to(top, (8, 128))
        scale = FULL / top

        @pl.loop(0, count)
        def _(i):
            k, c = i // per_share, lax.rem(i, per_share)
            value = read(s, p, 2 * k + 1 - bits[s], c) * scale
            q_send[s][p, k, :, pl.ds(pl.multiple_of(c * chunk, 128), chunk)] = (
                jnp.round(value).astype(jnp.int32).astype(jnp.int16)
            )

        where = {"seq": peers[s]}
        m_copies[s, p] = start(
            remote(m_send[s].at[p], m_recv[s].at[p], m_ss.at[s, p], m_rs.at[s, p], where)
        )
        q_copies[s, p] = start(
            remote(q_send[s].at[p], q_recv[s].at[p], q_ss.at[s, p], q_rs.at[s, p], where)
        )

    for p in range(prompts):
        send_half(0, p)

    def fold_steps(s):
        d_copies[s].wait_recv()
        right = jnp.full((prompts, share_len), bits[s], jnp.int32) == 1

        @pl.loop(0, n >> (s + 1))
        def _(k):
            if s == 0:
                own = steps[:, lanes(2 * k + bits[0])] * usable_rows
            else:
                own = d_cur[s - 1][2 * k + bits[s]]
            other = d_recv[s][k]
            d_sel[s][k] = jnp.where(right, own, other)
            d_cur[s][k] = own + other

        if s + 1 < levels:

            @pl.loop(0, n >> (s + 2))
            def _(k):
                d_send[s + 1][k] = d_cur[s][2 * k + 1 - bits[s + 1]]

            start(d_copies[s + 1])

    fold_steps(0)

    for copy in cache_copies:
        copy.wait_recv()
    relays = []
    for k in range(1, nb):
        relays.append(
            start(
                remote(
                    arrived.at[b],
                    arrived.at[b],
                    relay_ss.at[k - 1],
                    relay_rs.at[k - 1],
                    {"batch": lax.rem(b + k, nb)},
                )
            )
        )
    for copy in relays:
        copy.wait_recv()

    def pick(r):
        slot = b * requests + r
        chosen, length, hits = jnp.int32(0), jnp.int32(0), jnp.int32(0)
        for p in range(all_prompts):
            hit = tslot[p] == slot
            chosen = jnp.where(hit, p, chosen)
            length = jnp.where(hit, plen[p], length)
            hits = jnp.where(hit, 1, hits)
        return chosen, hits, jnp.where(hits > 0, length, clen[r])

    shape3 = (positions, kv_heads, width)
    position = lax.broadcasted_iota(jnp.int32, shape3, 0) * n + me
    flat = positions * kv_heads
    column = lax.broadcasted_iota(jnp.int32, (heads, flat), 1)
    owner = lax.broadcasted_iota(jnp.int32, (heads, flat), 0) // group
    same_head = lax.rem(column, kv_heads) == owner
    column_position = (column // kv_heads) * n + me
    lane_id = lax.broadcasted_iota(jnp.int32, (heads, 128), 1)

    def attend(r, lse_all):
        chosen, hits, length = pick(r)
        fresh_limit = jnp.where(hits > 0, length, 0)
        new = arrived[chosen // prompts, :, lax.rem(chosen, prompts)].reshape(shape3).astype(jnp.float32)
        old = resident[r].astype(jnp.float32)
        x = jnp.where(position < fresh_limit, new, old)
        x = jnp.where(position < length, x, 0.0)
        x = jnp.where(position == length, token[r].astype(jnp.float32)[None], x)
        merged[r] = x.astype(jnp.bfloat16)
        x2 = x.reshape(flat, width)
        keys = x2[:, :head_dim].astype(jnp.bfloat16)
        values = x2[:, head_dim:].astype(jnp.bfloat16)
        score = lax.dot_general(
            queries[r], keys, (((1,), (1,)), ((), ())), preferred_element_type=jnp.float32
        ) * (1.0 / math.sqrt(head_dim))
        seen = same_head & (column_position <= length)
        score = jnp.where(seen, score, LOW)
        top = jnp.max(score, axis=1, keepdims=True)
        weight = jnp.where(seen, jnp.exp(score - top), 0.0)
        total = jnp.sum(weight, axis=1, keepdims=True)
        out = jnp.dot(weight.astype(jnp.bfloat16), values, preferred_element_type=jnp.float32)
        some = total > 0.0
        safe = jnp.where(some, total, 1.0)
        out = out / safe
        lse = jnp.where(some, top + jnp.log(safe), LOW)
        for j in range(n):
            osend[j, r] = out[j * own_heads : (j + 1) * own_heads]
        return jnp.where(lane_id == r, lse, lse_all)

    lse_all = lax.fori_loop(0, requests, attend, jnp.zeros((heads, 128), jnp.float32))
    for j in range(n):
        lse_send[j] = lse_all[j * own_heads : (j + 1) * own_heads]
    o_copies = []
    for k in range(1, n):
        to = lax.rem(me + k, n)
        o_copies.append(
            start(
                remote(
                    lse_send.at[to], lse_recv.at[me], l_ss.at[k - 1], l_rs.at[k - 1], {"seq": to}
                )
            )
        )
        o_copies.append(
            start(
                remote(osend.at[to], orecv.at[me], o_ss.at[k - 1], o_rs.at[k - 1], {"seq": to})
            )
        )
    lse_recv[me] = lse_send[me]
    orecv[me] = osend[me]

    for s in range(1, levels):
        fold_steps(s)

    hand_copies = []

    def fold(s, p):
        m_copies[s, p].wait_recv()
        q_copies[s, p].wait_recv()
        scale = m_recv[s][p][0:1, 0:1] * (1.0 / FULL)
        right = jnp.full((state_n, chunk), bits[s], jnp.int32) == 1
        below = lax.rem(me, 1 << (s + 1))

        @pl.loop(0, (n >> (s + 1)) * per_share)
        def _(i):
            k, c = i // per_share, lax.rem(i, per_share)
            at = pl.ds(pl.multiple_of(c * chunk, 128), chunk)
            other = q_recv[s][p, k, :, at].astype(jnp.int32).astype(jnp.float32) * scale
            own = read(s, p, 2 * k + bits[s], c)
            rate = rates[:, lanes(k * (1 << (s + 1)) + below, c, chunk)]
            decay = jnp.exp(-rate * d_sel[s][k, :, at][p : p + 1])
            early = jnp.where(right, other, own)
            late = jnp.where(right, own, other)
            folded = decay * early + late
            if s + 1 < levels:
                acc[p, k, :, at] = folded
            else:
                handed[first + p, :, at] = folded

        if s + 1 < levels:
            send_half(s + 1, p)
        else:
            for k in range(1, nb):
                hand_copies.append(
                    start(
                        remote(
                            handed.at[first + p],
                            handed.at[first + p],
                            hand_ss.at[k - 1, p],
                            hand_rs.at[k - 1, p],
                            {"batch": lax.rem(b + k, nb)},
                        )
                    )
                )

    for wave in range(prompts + levels - 1):
        for s in reversed(range(levels)):
            p = wave - s
            if 0 <= p < prompts:
                fold(s, p)

    for copy in o_copies:
        copy.wait_recv()
    lane3 = lax.broadcasted_iota(jnp.int32, (n, own_heads, 128), 2)
    for r in range(requests):
        lse = jnp.sum(jnp.where(lane3 == r, lse_recv[...], 0.0), axis=2, keepdims=True)
        share = jnp.exp(lse - jnp.max(lse, axis=0, keepdims=True))
        top = jnp.sum(share * orecv[:, r], axis=0)
        attention[r] = (top / jnp.sum(share, axis=0)).astype(jnp.bfloat16)

    for copy in hand_copies:
        copy.wait_recv()

    eye = lax.broadcasted_iota(jnp.int32, (state_n, state_n), 0) == lax.broadcasted_iota(
        jnp.int32, (state_n, state_n), 1
    )

    def as_column(row):
        spread = jnp.where(eye, jnp.broadcast_to(row, (state_n, state_n)), 0.0)
        return jnp.sum(spread, axis=1, keepdims=True)

    picks = [pick(r) for r in range(requests)]
    in_all, out_all = s_in[...], s_out[...]
    in_cols = [as_column(in_all[r : r + 1]) for r in range(requests)]
    out_cols = [as_column(out_all[r : r + 1]) for r in range(requests)]

    @pl.loop(0, per_share)
    def _(c):
        at = pl.ds(pl.multiple_of(c * chunk, 128), chunk)
        step_rows = dt[:, at]
        x_rows = inner[:, at].astype(jnp.float32)
        g = gate[:, at].astype(jnp.float32)
        rate = -rates[:, lanes(me, c, chunk)]
        push_rows = step_rows * x_rows
        out_rows = []
        for r in range(requests):
            chosen, hits, _ = picks[r]
            fresh = jnp.full((state_n, chunk), hits, jnp.int32) > 0
            begin = jnp.where(fresh, handed[chosen, :, at], rstates[r, :, at])
            after = jnp.exp(rate * step_rows[r : r + 1]) * begin
            after = after + push_rows[r : r + 1] * in_cols[r]
            nstates[r, :, at] = after
            out_rows.append(jnp.sum(out_cols[r] * after, axis=0, keepdims=True))
        read_out = jnp.concatenate(out_rows, axis=0) + skip[:, at] * x_rows
        mout[:, at] = (read_out * (g / (1.0 + jnp.exp(-g)))).astype(jnp.bfloat16)

    for copy in pending:
        copy.wait_send()


def local(
    n,
    nb,
    prompt_cache,
    prompt_states,
    block_steps,
    prompt_lengths,
    target_slots,
    cache_lengths,
    resident_cache,
    token_cache,
    queries,
    resident_states,
    decay_rates,
    step_sizes,
    inner_input,
    inner_gate,
    state_input,
    state_readout,
    skip_gain,
):
    levels = n.bit_length() - 1
    prompts, block_len, kv_heads, width = prompt_cache.shape
    requests, heads, head_dim = queries.shape
    state_n, channels = decay_rates.shape
    share = channels // n
    own_heads = heads // n
    positions = resident_cache.shape[1]
    all_prompts = prompts * nb
    f32, bf16, i16 = jnp.float32, jnp.bfloat16, jnp.int16
    vmem = pl.BlockSpec(memory_space=pltpu.VMEM)
    smem = pl.BlockSpec(memory_space=pltpu.SMEM)
    dma = pltpu.SemaphoreType.DMA
    halves = [n >> (s + 1) for s in range(levels)]
    scratch = [
        pltpu.VMEM((nb, n, prompts, block_len // n, kv_heads, width), bf16),
        pltpu.VMEM((n, prompts, block_len // n, kv_heads, width), bf16),
        pltpu.VMEM((all_prompts, state_n, share), f32),
        pltpu.VMEM((prompts, n // 2, state_n, share), f32),
        pltpu.VMEM((n, requests, own_heads, head_dim), f32),
        pltpu.VMEM((n, requests, own_heads, head_dim), f32),
        pltpu.VMEM((n, own_heads, 128), f32),
        pltpu.VMEM((n, own_heads, 128), f32),
    ]
    for _ in range(4):
        scratch += [pltpu.VMEM((h + 1, prompts, share), f32) for h in halves]
    for _ in range(2):
        scratch += [pltpu.VMEM((prompts, h, state_n, share), i16) for h in halves]
    for _ in range(2):
        scratch += [pltpu.VMEM((prompts, 8, 128), f32) for h in halves]
    scratch += [dma((n - 1,))] * 2
    scratch += [dma((max(nb - 1, 1),))] * 2
    scratch += [dma((levels,))] * 2
    scratch += [dma((levels, prompts))] * 4
    scratch += [dma((max(nb - 1, 1), prompts))] * 2
    scratch += [dma((n - 1,))] * 4
    merged, attention, next_states, mamba_output = pl.pallas_call(
        functools.partial(kernel, (n, nb, levels, block_len)),
        out_shape=(
            jax.ShapeDtypeStruct((requests, positions, kv_heads, width), bf16),
            jax.ShapeDtypeStruct((requests, own_heads, head_dim), bf16),
            jax.ShapeDtypeStruct((requests, state_n, share), f32),
            jax.ShapeDtypeStruct((requests, share), bf16),
        ),
        in_specs=[smem] * 3 + [vmem] * 14,
        out_specs=(vmem,) * 4,
        scratch_shapes=scratch,
        compiler_params=pltpu.CompilerParams(
            collective_id=0, has_side_effects=True, vmem_limit_bytes=48 << 20
        ),
    )(
        prompt_lengths,
        target_slots,
        cache_lengths,
        prompt_cache.reshape(prompts, block_len // n, n, kv_heads, width),
        prompt_states[:, 0],
        block_steps[:, 0],
        resident_cache[:, :, 0],
        token_cache,
        queries,
        resident_states,
        decay_rates,
        step_sizes,
        inner_input,
        inner_gate,
        state_input,
        state_readout,
        skip_gain[None],
    )
    return merged[:, :, None], attention, next_states, mamba_output


def solution(mesh):
    n, nb = mesh.shape["seq"], mesh.shape["batch"]
    return jax.shard_map(
        functools.partial(local, n, nb),
        mesh=mesh,
        in_specs=(
            P(("groups", "batch"), "seq", None, None),
            P(("groups", "batch"), "seq", None, None),
            P(("groups", "batch"), "seq", None),
            P("groups"),
            P("groups"),
            P(("groups", "batch")),
            P(("groups", "batch"), None, "seq", None, None),
            P(("groups", "batch"), None, None),
            P(("groups", "batch"), None, None),
            P(("groups", "batch"), None, "seq"),
            P(),
            P(("groups", "batch"), "seq"),
            P(("groups", "batch"), "seq"),
            P(("groups", "batch"), "seq"),
            P(("groups", "batch"), None),
            P(("groups", "batch"), None),
            P("seq"),
        ),
        out_specs=(
            P(("groups", "batch"), None, "seq", None, None),
            P(("groups", "batch"), "seq", None),
            P(("groups", "batch"), None, "seq"),
            P(("groups", "batch"), "seq"),
        ),
        check_vma=False,
    )
```

time: 314 us -> 84.1 us (0.27)
  waiting for transfers between devices: 230 us -> 0 us
  Pallas kernels: 0 us -> 66.3 us
  other arithmetic: 26.8 us -> 0 us
  starting transfers between devices: 19.2 us -> 0 us
  between operations: 14.1 us -> 0.66 us
  matrix products: 6.71 us -> 0 us
  local copies, waits for them, and re-layouts: 12.4 us -> 15.8 us
    all_gather x3 -> x0, waiting for transfers between devices: 89.5 us -> none  [the longest x1 73.9 us: carried_in(): everything = lax.all_gather(shard, axis)]
    reduce_scatter x1 -> x0, waiting for transfers between devices: 73.6 us -> none  [local(): lax.psum_scatter(decay_term(every_states[:, 0], behind, usable, decay_rat...]
    pallas_call x0 -> x1, Pallas kernels: none -> 66.3 us  [local(): pl.pallas_call(functools.partial(kernel, (n, nb, levels, block_len)), out...]
    all_to_all x4 -> x0, waiting for transfers between devices: 65.6 us -> none  [the longest x1 48.5 us: local(): lax.all_to_all(to_cyclic(every_cache, seq_count), 'seq', split_axis=2, co...]
    all_to_all x4 -> x0, starting transfers between devices: 19.1 us -> none  [the longest x1 5.95 us: local(): lax.all_to_all(denominator[:, None], 'seq', split_axis=2, concat_axis=1,...]
    select_n x11 -> x0, other arithmetic: 13.4 us -> none  [the longest x8 9.73 us: step(): return jnp.where(reached, new, before)]
    unnamed x42 -> x33, local copies, waits for them, and re-layouts: 3.74 us -> 15.8 us
    mul x3 -> x0, other arithmetic: 7.25 us -> none  [the longest x1 6.18 us: decay_term(): usable[:, None, None] * jnp.exp(-rates[None] * behind[:, None, :]) * states]
  transfers between devices with their start and end apart: 8 -> 0, of which waited for: 8 -> 0; matrix products, arithmetic and copies ran while one was open for 12% -> 0% of each run, Pallas kernels for 0% -> 0%
where the time goes in v1:
time: 84.1 us; the launch traced here: 82.8 us
  Pallas kernels  66.3 us (79%)
  local copies, waits for them, and re-layouts  15.8 us (19%)
    pallas_call x1, Pallas kernels, local(): pl.pallas_call(functools.partial(kernel, (n, nb, levels, block_len)), out...  66.3 us
    unnamed x33, local copies, waits for them, and re-layouts  15.8 us

profile of v1, /device:TPU:0, one launch (start us, length us, event | category | flops | bytes accessed | tf_op | source)
XLA Modules:
  0.0 82.8 jit_solution(18182566441382505397)
XLA Ops:
  0.6 1.1 %copy.24 = f32[4,1,16384]{2,0,1:T(4,128)S(1)} copy(f32[4,1,16384]{2,1,0:T(1,128)} %param.19) | data formatting | bytes 524288
  1.8 0.0 copy-start
  1.8 1.2 %copy-done = bf16[8,32,1,8,256]{4,3,2,1,0:T(8,128)(2,1)S(1)} copy-done((bf16[8,32,1,8,256]{4,3,2,1,0:T(8,128)(2,1)S(1)}, bf16[8,32,1,8,256]{4,3,2,1,0:T(8,128)(2,1)}, u32[]{:S(2)}) %copy-start) | copy-done | bytes 1048600
  3.0 0.0 copy-start.1
  3.0 1.2 %copy-done.1 = f32[8,16,2048]{2,1,0:T(8,128)S(1)} copy-done((f32[8,16,2048]{2,1,0:T(8,128)S(1)}, f32[8,16,2048]{2,1,0:T(8,128)}, u32[]{:S(2)}) %copy-start.1) | copy-done | bytes 1048600
  4.2 0.0 copy-start.2
  4.2 1.0 %copy-done.2 = bf16[4,32,8,256]{3,2,1,0:T(8,128)(2,1)S(1)} copy-done((bf16[4,32,8,256]{3,2,1,0:T(8,128)(2,1)S(1)}, bf16[4,32,8,256]{3,2,1,0:T(8,128)(2,1)}, u32[]{:S(2)}) %copy-start.2) | copy-done | bytes 524312
  5.3 0.0 copy-start.3
  5.3 0.9 %copy-done.3 = bf16[8,64,128]{2,1,0:T(8,128)(2,1)S(1)} copy-done((bf16[8,64,128]{2,1,0:T(8,128)(2,1)S(1)}, bf16[8,64,128]{2,1,0:T(8,128)(2,1)}, u32[]{:S(2)}) %copy-start.3) | copy-done | bytes 131096
  6.2 0.0 copy-start.4
  6.2 0.8 %copy-done.4 = f32[8,2048]{1,0:T(8,128)S(1)} copy-done((f32[8,2048]{1,0:T(8,128)S(1)}, f32[8,2048]{1,0:T(8,128)}, u32[]{:S(2)}) %copy-start.4) | copy-done | bytes 65560
  7.0 0.0 copy-start.5
  7.0 0.8 copy-done.5
  7.8 0.0 copy-start.6
  7.8 0.8 copy-done.6
  8.5 0.0 copy-start.7
  8.5 0.8 copy-done.7
  9.3 0.0 copy-start.8
  9.3 0.7 copy-done.8
  10.0 0.0 copy-start.9
  10.0 0.7 copy-done.9
  10.7 0.0 copy-start.10
  10.7 0.7 copy-done.10
  11.3 0.0 copy-start.11
  11.3 0.7 copy-done.11
  12.0 0.0 copy-start.12
  12.0 0.7 copy-done.12
  12.7 0.0 copy-start.13
  12.7 0.7 copy-done.13
  13.3 66.3 %shard_map.192 = (bf16[8,32,8,256]{3,2,1,0:T(8,128)(2,1)S(1)}, bf16[8,8,128]{2,1,0:T(8,128)(2,1)S(1)}, f32[8,16,2048]{2,1,0:T(8,128)S(1)}, bf16[8,2048]{1,0:T(8,128)(2,1)S(1)}) custom-call(s32[8]{0:T(128)S(1)} %copy-done.11, s32[8]{0:T(128)S(1)} %copy-done.12, s32[8]{0:T(128)S(1)} %copy-done.13, bf16[4,4,8,8,256]{4,3,2,1,0:T(8,128)(2,1)S(1)} %bitcast.13, ...), custom_call_target="tpu_custom_call" | custom-call | tf_op jit(solution)/shard_map/pallas_call | solution.py:449
  79.6 1.0 %copy.29 = bf16[8,32,1,8,256]{4,3,2,1,0:T(8,128)(2,1)} copy(bf16[8,32,1,8,256]{4,3,2,1,0:T(8,128)(2,1)S(1)} %bitcast.12) | data formatting | bytes 2097152
  80.6 0.6 copy.30
  81.2 1.0 %copy.31 = f32[8,16,2048]{2,1,0:T(8,128)} copy(f32[8,16,2048]{2,1,0:T(8,128)S(1)} %get-tuple-element.22) | data formatting | bytes 2097152
  82.2 0.6 copy.32
Async XLA Ops:
  1.8 1.2 %copy-start = (bf16[8,32,1,8,256]{4,3,2,1,0:T(8,128)(2,1)S(1)}, bf16[8,32,1,8,256]{4,3,2,1,0:T(8,128)(2,1)}, u32[]{:S(2)}) copy-start(bf16[8,32,1,8,256]{4,3,2,1,0:T(8,128)(2,1)} %param.23) | copy-start | bytes 3145732
  3.0 1.2 %copy-start.1 = (f32[8,16,2048]{2,1,0:T(8,128)S(1)}, f32[8,16,2048]{2,1,0:T(8,128)}, u32[]{:S(2)}) copy-start(f32[8,16,2048]{2,1,0:T(8,128)} %rstates.1) | copy-start | bytes 3145732
  4.2 1.0 %copy-start.2 = (bf16[4,32,8,256]{3,2,1,0:T(8,128)(2,1)S(1)}, bf16[4,32,8,256]{3,2,1,0:T(8,128)(2,1)}, u32[]{:S(2)}) copy-start(bf16[4,32,8,256]{3,2,1,0:T(8,128)(2,1)} %param.17) | copy-start | bytes 1572868
  5.3 0.9 %copy-start.3 = (bf16[8,64,128]{2,1,0:T(8,128)(2,1)S(1)}, bf16[8,64,128]{2,1,0:T(8,128)(2,1)}, u32[]{:S(2)}) copy-start(bf16[8,64,128]{2,1,0:T(8,128)(2,1)} %queries.1) | copy-start | bytes 393220
  6.2 0.8 %copy-start.4 = (f32[8,2048]{1,0:T(8,128)S(1)}, f32[8,2048]{1,0:T(8,128)}, u32[]{:S(2)}) copy-start(f32[8,2048]{1,0:T(8,128)} %dt.1) | copy-start | bytes 196612
  7.0 0.8 copy-start.5
  7.8 0.8 copy-start.6
  8.5 0.8 copy-start.7
  9.3 0.7 copy-start.8
  10.0 0.7 copy-start.9
  10.7 0.7 copy-start.10
  11.3 0.7 copy-start.11
  12.0 0.7 copy-start.12
  12.7 0.7 copy-start.13
